TPU v7x, 32 devices: a whole 2x2x4 slice. The times are simulated.
32 devices in a mesh: row: 8 (over y, x, core), col: 4 (over z).
Axes of the slice: x: 2, y: 2, z: 4, core: 2. Of those that a mesh axis runs over, the one named last changes fastest.
Arguments:
- tokens: bfloat16 [48, 8192], P('row', 'col'), may hold values from -6 to 6
- gate_weight: bfloat16 [8192, 20480], P('col', 'row'), may hold values from -0.0625 to 0.0625
- up_weight: bfloat16 [8192, 20480], P('col', 'row'), may hold values from -0.0625 to 0.0625
- down_weight: bfloat16 [20480, 8192], P('row', 'col'), may hold values from -0.0390625 to 0.0390625
- keep_mask: int32 [48, 20480], P('col', 'row'), may hold values 0 or 1
- cotangent: bfloat16 [48, 8192], P('row', 'col'), may hold values from -6 to 6
Outputs:
- mixed_out: bfloat16 [48, 8192], P('row', 'col')
- input_grad: bfloat16 [48, 8192], P('row', 'col')
- gate_grad: bfloat16 [8192, 20480], P('col', 'row')
- up_grad: bfloat16 [8192, 20480], P('col', 'row')
- down_grad: bfloat16 [20480, 8192], P('row', 'col')
All inputs are finite; a program needn't handle non-finite values. No bound on the sum of `keep_mask` on one device may be relied on, other than what follows from the above.
Results may differ from a plain program's by a relative error of at most 0.0049.
Values may be sent and summed in bfloat16 or wider, within the bound.
A program may use at most 128 MiB of HBM per device.

v0:
```python
import jax
import jax.numpy as jnp
from jax import lax
from jax.sharding import PartitionSpec as P

keep_scale = 1.0 / 0.9
contract_last = (((1,), (1,)), ((), ()))
contract_first = (((0,), (0,)), ((), ()))


def project_in(tokens, gate_weight, up_weight):
    gathered = lax.all_gather(tokens, "row", axis=0, tiled=True)
    gate_part = jnp.dot(gathered, gate_weight, preferred_element_type=jnp.float32)
    up_part = jnp.dot(gathered, up_weight, preferred_element_type=jnp.float32)
    gate_value, up_value = lax.psum((gate_part, up_part), "col")
    return (gathered, gate_value, up_value)


def body(tokens, gate_weight, up_weight, down_weight, keep_mask, cotangent):
    gathered, gate_value, up_value = project_in(tokens, gate_weight, up_weight)
    mask_all = lax.all_gather(keep_mask, "col", axis=0, tiled=True)
    keep_factor = mask_all.astype(jnp.float32) * keep_scale
    sigmoid_gate = jax.nn.sigmoid(gate_value)
    silu_gate = gate_value * sigmoid_gate
    hidden = (silu_gate * up_value * keep_factor).astype(jnp.bfloat16)
    mixed_out = lax.psum_scatter(
        jnp.dot(hidden, down_weight, preferred_element_type=jnp.float32),
        "row",
        scatter_dimension=0,
        tiled=True,
    ).astype(jnp.bfloat16)
    cot_all = lax.all_gather(cotangent, "row", axis=0, tiled=True)
    hidden_part = lax.dot_general(
        cot_all, down_weight, contract_last, preferred_element_type=jnp.float32
    )
    grad_hidden = lax.psum(hidden_part, "col")
    down_grad = lax.dot_general(
        hidden, cot_all, contract_first, preferred_element_type=jnp.float32
    ).astype(jnp.bfloat16)
    gathered, gate_value, up_value = project_in(tokens, gate_weight, up_weight)
    sigmoid_gate = jax.nn.sigmoid(gate_value)
    silu_gate = gate_value * sigmoid_gate
    grad_pre = grad_hidden * keep_factor
    grad_gate = (
        grad_pre * up_value * sigmoid_gate * (1.0 + gate_value * (1.0 - sigmoid_gate))
    ).astype(jnp.bfloat16)
    grad_up = (grad_pre * silu_gate).astype(jnp.bfloat16)
    gate_all, up_all = (grad_gate, grad_up)
    gate_grad = lax.dot_general(
        gathered, gate_all, contract_first, preferred_element_type=jnp.float32
    ).astype(jnp.bfloat16)
    up_grad = lax.dot_general(
        gathered, up_all, contract_first, preferred_element_type=jnp.float32
    ).astype(jnp.bfloat16)
    first = lax.dot_general(
        gate_all, gate_weight, contract_last, preferred_element_type=jnp.float32
    )
    second = lax.dot_general(up_all, up_weight, contract_last, preferred_element_type=jnp.float32)
    input_grad = lax.psum_scatter(first + second, "row", scatter_dimension=0, tiled=True).astype(
        jnp.bfloat16
    )
    return (mixed_out, input_grad, gate_grad, up_grad, down_grad)


def solution(mesh):
    placed = (
        P("row", "col"),
        P("col", "row"),
        P("col", "row"),
        P("row", "col"),
        P("col", "row"),
        P("row", "col"),
    )
    return jax.shard_map(
        body,
        mesh=mesh,
        in_specs=placed,
        out_specs=(
            P("row", "col"),
            P("row", "col"),
            P("col", "row"),
            P("col", "row"),
            P("row", "col"),
        ),
        check_vma=False,
    )
```

profile of v0, /device:TPU:0, one launch (start us, length us, event | category | flops | bytes accessed | tf_op | source)
XLA Modules:
  0.0 219.4 jit_solution(4563992765562705758)
XLA Ops:
  7.2 0.0 all-reduce.8.cloned.1.call-start
  7.2 11.0 %all-gather = bf16[8,6,2048]{2,1,0:T(8,128)(2,1)S(1)} all-gather(bf16[1,6,2048]{2,1,0:T(8,128)(2,1)} %bitcast.34), channel_id=1, replica_groups=mesh['row'=8,'col'=4] {'row'}, dimensions={0}, use_global_device_ids=true | all-gather | bytes 221184 | tf_op jit(solution)/shard_map/all_gather | solution.py:12
  18.2 0.1 reshape.11
  18.3 6.8 %fusion.6 = f32[48,2560]{1,0:T(8,128)} fusion(bf16[48,2048]{1,0:T(8,128)(2,1)S(1)} %reshape.11, bf16[2048,2560]{1,0:T(8,128)(2,1)} %param.7), kind=kOutput, calls=%fused_computation.14 | convolution fusion | flops 503316480 | bytes 11173888 | tf_op jit(solution)/shard_map/dot_general | solution.py:13
  25.1 0.2 copy-done
  25.3 2.6 %fusion.7 = f32[48,2560]{1,0:T(8,128)} fusion(bf16[48,2048]{1,0:T(8,128)(2,1)S(1)} %reshape.11, bf16[2048,2560]{1,0:T(8,128)(2,1)S(1)} %copy-done), kind=kOutput, calls=%fused_computation.15 | convolution fusion | flops 503316480 | bytes 11173888 | tf_op jit(solution)/shard_map/dot_general | solution.py:14
  27.9 9.2 %all-gather.2 = bf16[8,6,2048]{2,1,0:T(8,128)(2,1)S(1)} all-gather(bf16[1,6,2048]{2,1,0:T(8,128)(2,1)S(1)} %bitcast.35), channel_id=1, replica_groups=mesh['row'=8,'col'=4] {'row'}, dimensions={0}, use_global_device_ids=true | all-gather | bytes 221184 | tf_op jit(solution)/shard_map/all_gather | solution.py:32
  37.1 0.1 reshape.15
  37.2 8.0 %fusion.9 = f32[48,2560]{1,0:T(8,128)} fusion(bf16[48,2048]{1,0:T(8,128)(2,1)S(1)} %reshape.15, bf16[2560,2048]{1,0:T(8,128)(2,1)} %param.9), kind=kOutput, calls=%fused_computation.17 | convolution fusion | flops 503316480 | bytes 11173888 | tf_op jit(solution)/shard_map/dot_general | solution.py:33
  45.2 25.6 %all-gather.1 = s32[4,12,2560]{2,1,0:T(8,128)S(1)} all-gather(s32[1,12,2560]{2,1,0:T(8,128)S(1)} %bitcast.33), channel_id=1, replica_groups=mesh['row'=8,'col'=4] {'col'}, dimensions={0}, use_global_device_ids=true | all-gather | bytes 614400 | tf_op jit(solution)/shard_map/all_gather | solution.py:21
  70.9 0.1 convert_multiply_fusion
  70.9 0.1 reshape.18
  71.0 0.6 dynamic-slice.6
  72.2 46.9 %all-reduce.8.cloned.1.call-done = (f32[48,2560]{1,0:T(8,128)}, f32[48,2560]{1,0:T(8,128)}, f32[48,2560]{1,0:T(8,128)}) async-done(((f32[48,2560]{1,0:T(8,128)}, f32[48,2560]{1,0:T(8,128)}, f32[48,2560]{1,0:T(8,128)}), (f32[48,2560]{1,0:T(8,128)}, f32[48,2560]{1,0:T(8,128)}, f32[48,2560]{1,0:T(8,128)})) %all-reduce.8.cloned.1.call-update) | async-done | bytes 1474576 | tf_op jit(solution)/shard_map/psum | solution.py:15
  119.1 1.6 multiply_convert_fusion
  120.7 7.3 %fusion.10 = f32[48,2048]{1,0:T(8,128)S(1)} fusion(bf16[48,2560]{1,0:T(8,128)(2,1)S(1)} %get-tuple-element.28, bf16[2048,2560]{1,0:T(8,128)(2,1)} %param.7), kind=kOutput, calls=%fused_computation.18 | convolution fusion | flops 503316480 | bytes 11124736 | tf_op jit(solution)/shard_map/dot_general | solution.py:55
  128.0 6.1 %fusion.8 = f32[48,2048]{1,0:T(8,128)S(1)} fusion(bf16[48,2560]{1,0:T(8,128)(2,1)S(1)} %get-tuple-element.29, bf16[2560,2048]{1,0:T(8,128)(2,1)} %param.9), kind=kOutput, calls=%fused_computation.16 | convolution fusion | flops 503316480 | bytes 11124736 | tf_op jit(solution)/shard_map/dot_general | solution.py:27
  134.1 3.2 %convolution_add_fusion = f32[48,2048]{1,0:T(8,128)S(1)} fusion(f32[48,2048]{1,0:T(8,128)S(1)} %fusion.10, bf16[48,2560]{1,0:T(8,128)(2,1)S(1)} %get-tuple-element.27, bf16[2048,2560]{1,0:T(8,128)(2,1)S(1)} %bitcast.32), kind=kOutput, calls=%fused_computation.5 | convolution fusion | flops 503414784 | bytes 11517952 | tf_op jit(solution)/shard_map/dot_general | solution.py:58
  137.3 19.5 %fusion.5 = (f32[8,2048]{1,0:T(8,128)S(1)}, f32[8,2048]{1,0:T(8,128)S(1)}) fusion(f32[48,2048]{1,0:T(8,128)S(1)} %fusion.8, f32[48,2048]{1,0:T(8,128)S(1)} %convolution_add_fusion), kind=kCustom, calls=%all-reduce-scatter.2 | all-reduce-scatter fusion | flops 262145 | bytes 918016
  156.8 5.7 %fusion.2 = bf16[2048,2560]{0,1:T(8,128)(2,1)} fusion(bf16[48,2560]{1,0:T(8,128)(2,1)S(1)} %get-tuple-element.28, bf16[48,2048]{1,0:T(8,128)(2,1)S(1)} %reshape.11), kind=kOutput, calls=%fused_computation.3 | convolution fusion | flops 508559360 | bytes 10928128 | tf_op jit(solution)/shard_map/dot_general | solution.py:49
  162.5 5.5 %fusion.3 = bf16[2048,2560]{0,1:T(8,128)(2,1)} fusion(bf16[48,2560]{1,0:T(8,128)(2,1)S(1)} %get-tuple-element.27, bf16[48,2048]{1,0:T(8,128)(2,1)S(1)} %reshape.11), kind=kOutput, calls=%fused_computation.4 | convolution fusion | flops 508559360 | bytes 10928128 | tf_op jit(solution)/shard_map/dot_general | solution.py:52
  168.0 1.3 collective-permute-start.2
  169.3 1.3 collective-permute-start.3
  170.6 5.7 %convolution_convert_fusion = bf16[2560,2048]{1,0:T(8,128)(2,1)} fusion(bf16[48,2560]{1,0:T(8,128)(2,1)S(1)} %get-tuple-element.29, bf16[48,2048]{1,0:T(8,128)(2,1)S(1)} %reshape.15), kind=kOutput, calls=%fused_computation | convolution fusion | flops 508559360 | bytes 10928128 | tf_op jit(solution)/shard_map/dot_general | solution.py:37
  176.3 4.5 %collective-permute-start = (bf16[8,2048]{1,0:T(8,128)(2,1)S(1)}, bf16[8,2048]{1,0:T(8,128)(2,1)S(1)}, u32[]{:S(2)}, u32[]{:S(2)}) collective-permute-start(bf16[8,2048]{1,0:T(8,128)(2,1)S(1)} %convert), channel_id=1, source_target_pairs={{0,4},{4,8},{8,12},{12,16},{16,20},{20,24},{24,28},{1,5},{5,9},{9,... | collective-permute-start | bytes 98312
  180.8 2.5 %collective-permute-start.1 = (bf16[6,2048]{1,0:T(8,128)(2,1)S(1)}, bf16[6,2048]{1,0:T(8,128)(2,1)S(1)}, u32[]{:S(2)}, u32[]{:S(2)}) collective-permute-start(bf16[6,2048]{1,0:T(8,128)(2,1)S(1)} %slice), channel_id=1, source_target_pairs={{0,8},{4,12},{8,16},{12,20},{16,24},{20,28},{1,9},{5,13},{9,17},{1... | collective-permute-start | bytes 73736
  183.3 13.7 %copy.15 = bf16[2048,2560]{1,0:T(8,128)(2,1)} copy(bf16[2048,2560]{0,1:T(8,128)(2,1)} %fusion.2) | data formatting | bytes 20971520
  197.0 13.7 %copy.16 = bf16[2048,2560]{1,0:T(8,128)(2,1)} copy(bf16[2048,2560]{0,1:T(8,128)(2,1)} %fusion.3) | data formatting | bytes 20971520
  210.7 0.3 concatenate.1
  211.0 0.6 dynamic-slice_convert_fusion
  211.6 0.3 concatenate
  211.9 0.6 dynamic-slice_convert_fusion.1
  (23 shorter events, 0.1 us)
Async XLA Ops:
  7.2 111.9 %all-reduce.8.cloned.1.call-start = ((), (), s32[]{:S(2)}) async-start(), calls=%async_computation | async-start | bytes 2949120 | tf_op jit(solution)/shard_map/psum | solution.py:15
  18.3 7.0 %copy-start = (bf16[2048,2560]{1,0:T(8,128)(2,1)S(1)}, bf16[2048,2560]{1,0:T(8,128)(2,1)}, u32[]{:S(2)}) copy-start(bf16[2048,2560]{1,0:T(8,128)(2,1)} %param.8) | copy-start | bytes 31457284
  25.3 2.6 %copy-start.2 = (bf16[6,2048]{1,0:T(8,128)(2,1)S(1)}, bf16[6,2048]{1,0:T(8,128)(2,1)}, u32[]{:S(2)}) copy-start(bf16[6,2048]{1,0:T(8,128)(2,1)} %param.11) | copy-start | bytes 73732
  27.9 17.3 %copy-start.1 = (s32[12,2560]{1,0:T(8,128)S(1)}, s32[12,2560]{1,0:T(8,128)}, u32[]{:S(2)}) copy-start(s32[12,2560]{1,0:T(8,128)} %param.10) | copy-start | bytes 368644
  27.9 43.1 %copy-start.3 = (u32[32]{0:T(128)S(1)}, u32[32]{0:T(128)}, u32[]{:S(2)}) copy-start(u32[32]{0:T(128)} %constant.8) | copy-start | bytes 388
  120.7 13.4 %slice-start = ((s8[10485760]{0:T(1024)(128)(4,1)}), s8[4194304]{0:T(1024)(128)(4,1)S(1)}, s32[]{:S(2)}) async-start(s8[10485760]{0:T(1024)(128)(4,1)} %bitcast.31), calls=%async_computation.1 | async-start | bytes 8388608
  120.7 13.4 %slice-start.1 = ((s8[10485760]{0:T(1024)(128)(4,1)}), s8[4194304]{0:T(1024)(128)(4,1)S(1)}, s32[]{:S(2)}) async-start(s8[10485760]{0:T(1024)(128)(4,1)} %bitcast.31), calls=%async_computation.2 | async-start | bytes 8388608
  128.0 6.1 %slice-start.2 = ((s8[10485760]{0:T(1024)(128)(4,1)}), s8[2097152]{0:T(1024)(128)(4,1)S(1)}, s32[]{:S(2)}) async-start(s8[10485760]{0:T(1024)(128)(4,1)} %bitcast.31), calls=%async_computation.3 | async-start | bytes 4194304
  168.0 42.7 %collective-permute-start.2 = (bf16[8,2048]{1,0:T(8,128)(2,1)S(1)}, bf16[8,2048]{1,0:T(8,128)(2,1)S(1)}, u32[]{:S(2)}, u32[]{:S(2)}) collective-permute-start(bf16[8,2048]{1,0:T(8,128)(2,1)S(1)} %convert.1), channel_id=1, source_target_pairs={{0,4},{4,8},{8,12},{12,16},{16,20},{20,24},{24,28},{1,5},{5,9},{9,... | collective-permute-start | bytes 98312
  169.3 41.4 %collective-permute-start.3 = (bf16[6,2048]{1,0:T(8,128)(2,1)S(1)}, bf16[6,2048]{1,0:T(8,128)(2,1)S(1)}, u32[]{:S(2)}, u32[]{:S(2)}) collective-permute-start(bf16[6,2048]{1,0:T(8,128)(2,1)S(1)} %slice.1), channel_id=1, source_target_pairs={{0,8},{4,12},{8,16},{12,20},{16,24},{20,28},{1,9},{5,13},{9,17},{1... | collective-permute-start | bytes 73736
  176.3 35.4 %collective-permute-start = (bf16[8,2048]{1,0:T(8,128)(2,1)S(1)}, bf16[8,2048]{1,0:T(8,128)(2,1)S(1)}, u32[]{:S(2)}, u32[]{:S(2)}) collective-permute-start(bf16[8,2048]{1,0:T(8,128)(2,1)S(1)} %convert), channel_id=1, source_target_pairs={{0,4},{4,8},{8,12},{12,16},{16,20},{20,24},{24,28},{1,5},{5,9},{9,... | collective-permute-start | bytes 98312
  180.8 30.8 %collective-permute-start.1 = (bf16[6,2048]{1,0:T(8,128)(2,1)S(1)}, bf16[6,2048]{1,0:T(8,128)(2,1)S(1)}, u32[]{:S(2)}, u32[]{:S(2)}) collective-permute-start(bf16[6,2048]{1,0:T(8,128)(2,1)S(1)} %slice), channel_id=1, source_target_pairs={{0,8},{4,12},{8,16},{12,20},{16,24},{20,28},{1,9},{5,13},{9,17},{1... | collective-permute-start | bytes 73736
Sparse Core Ops, SparseCore 0:
  45.3 73.7 all-reduce.7
where the time goes:
time: 220 us; the launch traced here: 219 us
  blocking collectives  65.3 us (30%)
  matrix products  50.7 us (23%)
  waiting for transfers between devices  46.9 us (21%)
  local copies, waits for them, and re-layouts  30.2 us (14%)
  between operations  14.9 us (7%)
  starting transfers between devices  9.62 us (4%)
    psum x1, waiting for transfers between devices, project_in(): gate_value, up_value = lax.psum((gate_part, up_part), 'col')  46.9 us
    unnamed x23, local copies, waits for them, and re-layouts  28.9 us
    all_gather x1, blocking collectives, body(): mask_all = lax.all_gather(keep_mask, 'col', axis=0, tiled=True)  25.6 us
    unnamed x1, blocking collectives  19.5 us
    all_gather x1, blocking collectives, project_in(): gathered = lax.all_gather(tokens, 'row', axis=0, tiled=True)  11 us
    unnamed x4, starting transfers between devices  9.59 us
    all_gather x1, blocking collectives, body(): cot_all = lax.all_gather(cotangent, 'row', axis=0, tiled=True)  9.18 us
    dot_general x1, matrix products, body(): lax.dot_general(cot_all, down_weight, contract_last, preferred_element_ty...  8.01 us
  transfers between devices with their start and end apart: 5, of which 1 were waited for; matrix products, arithmetic and copies ran while one was open for 16% of the time, Pallas kernels for 0%

commit v1 on v0

v1 whole, which is shorter than its diff:
```python
import functools

import jax
import jax.numpy as jnp
from jax import lax
from jax.experimental import pallas as pl
from jax.experimental.pallas import tpu as pltpu
from jax.sharding import PartitionSpec as P

keep_scale = 1.0 / 0.9
contract_last = (((1,), (1,)), ((), ()))
contract_first = (((0,), (0,)), ((), ()))
f32 = jnp.float32
bf16 = jnp.bfloat16
MESH = pl.DeviceIdType.MESH


def project_in(tokens, gate_weight, up_weight):
    gathered = lax.all_gather(tokens, "row", axis=0, tiled=True)
    gate_part = jnp.dot(gathered, gate_weight, preferred_element_type=f32)
    up_part = jnp.dot(gathered, up_weight, preferred_element_type=f32)
    gate_value, up_value = lax.psum((gate_part, up_part), "col")
    return (gathered, gate_value, up_value)


def plain_body(tokens, gate_weight, up_weight, down_weight, keep_mask, cotangent):
    gathered, gate_value, up_value = project_in(tokens, gate_weight, up_weight)
    mask_all = lax.all_gather(keep_mask, "col", axis=0, tiled=True)
    keep_factor = mask_all.astype(f32) * keep_scale
    sigmoid_gate = jax.nn.sigmoid(gate_value)
    silu_gate = gate_value * sigmoid_gate
    hidden = (silu_gate * up_value * keep_factor).astype(bf16)
    mixed_out = lax.psum_scatter(
        jnp.dot(hidden, down_weight, preferred_element_type=f32),
        "row",
        scatter_dimension=0,
        tiled=True,
    ).astype(bf16)
    cot_all = lax.all_gather(cotangent, "row", axis=0, tiled=True)
    hidden_part = lax.dot_general(cot_all, down_weight, contract_last, preferred_element_type=f32)
    grad_hidden = lax.psum(hidden_part, "col")
    down_grad = lax.dot_general(
        hidden, cot_all, contract_first, preferred_element_type=f32
    ).astype(bf16)
    grad_pre = grad_hidden * keep_factor
    grad_gate = (
        grad_pre * up_value * sigmoid_gate * (1.0 + gate_value * (1.0 - sigmoid_gate))
    ).astype(bf16)
    grad_up = (grad_pre * silu_gate).astype(bf16)
    gate_grad = lax.dot_general(
        gathered, grad_gate, contract_first, preferred_element_type=f32
    ).astype(bf16)
    up_grad = lax.dot_general(
        gathered, grad_up, contract_first, preferred_element_type=f32
    ).astype(bf16)
    first = lax.dot_general(grad_gate, gate_weight, contract_last, preferred_element_type=f32)
    second = lax.dot_general(grad_up, up_weight, contract_last, preferred_element_type=f32)
    input_grad = lax.psum_scatter(first + second, "row", scatter_dimension=0, tiled=True).astype(
        bf16
    )
    return (mixed_out, input_grad, gate_grad, up_grad, down_grad)


def one_hot(rows, cols, want):
    i = lax.broadcasted_iota(jnp.int32, (rows, cols), 0)
    j = lax.broadcasted_iota(jnp.int32, (rows, cols), 1)
    return jnp.where(want(i, j), 1.0, 0.0).astype(bf16)


def layer_kernel(R, C, tok_ref, cot_ref, mask_ref, gate_hbm, up_hbm, down_hbm,
                 mixed_ref, input_ref, tok_all, cot_all, act,
                 wgate, wup, wdown, wsem, pack, packed, gathered, x_send, x_recv,
                 mpad, mpacked, mall, m_send, m_recv,
                 part32, own, gh_out, gh_in, gu_in, p_send, p_recv,
                 a_send, a_recv, acc, rs_out, rs_in, r_send, r_recv):
    me_r = lax.axis_index("row")
    me_c = lax.axis_index("col")
    t, D = tok_ref.shape
    F = gate_hbm.shape[1]
    S = F // C
    T = R * t
    tm = mask_ref.shape[0]

    def peer_c(j):
        return lax.rem(me_c + 1 + j, C)

    def cols(p):
        return pl.ds(pl.multiple_of(p * S, 128), S)

    def weight_copy(a, j):
        p = peer_c(j)
        src, dst = ((down_hbm.at[cols(p), :], wdown), (gate_hbm.at[:, cols(p)], wgate),
                    (up_hbm.at[:, cols(p)], wup))[a]
        return pltpu.make_async_copy(src, dst.at[j], wsem.at[a, j])

    for a in range(3):
        for j in range(C):
            weight_copy(a, j).start()

    barrier = pltpu.get_barrier_semaphore()
    for k in range(1, R):
        pl.semaphore_signal(barrier, inc=1, device_id={"row": lax.rem(me_r + k, R)}, device_id_type=MESH)
    for k in range(1, C):
        pl.semaphore_signal(barrier, inc=1, device_id={"col": lax.rem(me_c + k, C)}, device_id_type=MESH)

    pack[...] = jnp.zeros_like(pack)
    pack[0:t, :] = tok_ref[...].astype(f32)
    pack[8:8 + t, :] = cot_ref[...].astype(f32)
    mine = pack[...].astype(bf16)
    packed[...] = mine
    gathered[me_r] = mine
    mpad[...] = jnp.zeros_like(mpad)
    mpad[0:tm, :] = mask_ref[...].astype(f32)
    mpacked[...] = mpad[...].astype(bf16)
    mall[me_c] = mpacked[:, cols(me_c)]

    pl.semaphore_wait(barrier, R - 1 + C - 1)

    def x_copy(k):
        return pltpu.make_async_remote_copy(
            src_ref=packed, dst_ref=gathered.at[me_r], send_sem=x_send.at[k], recv_sem=x_recv.at[k],
            device_id={"row": lax.rem(me_r + k, R)}, device_id_type=MESH)

    def m_copy(k):
        p = lax.rem(me_c + k, C)
        return pltpu.make_async_remote_copy(
            src_ref=mpacked.at[:, cols(p)], dst_ref=mall.at[me_c], send_sem=m_send.at[k],
            recv_sem=m_recv.at[k], device_id={"col": p}, device_id_type=MESH)

    for k in range(1, R):
        x_copy(k).start()
    for k in range(1, C):
        m_copy(k).start()
    for k in range(1, R):
        x_copy(k).wait_recv()

    flat = gathered[...].reshape(R * 16, D)
    pick = one_hot(T, R * 16, lambda i, j: j == (i // t) * 16 + i % t)
    tok_all[...] = jnp.dot(pick, flat, preferred_element_type=f32).astype(bf16)
    pick = one_hot(T, R * 16, lambda i, j: j == (i // t) * 16 + 8 + i % t)
    cot_all[...] = jnp.dot(pick, flat, preferred_element_type=f32).astype(bf16)

    def part_copy(a, j):
        src, dst = ((gh_out.at[j], gh_in.at[me_c]), (part32.at[0, j], gu_in.at[0, me_c]),
                    (part32.at[1, j], gu_in.at[1, me_c]))[a]
        return pltpu.make_async_remote_copy(
            src_ref=src, dst_ref=dst, send_sem=p_send.at[a, j], recv_sem=p_recv.at[a, j],
            device_id={"col": peer_c(j)}, device_id_type=MESH)

    def partial(a, j):
        weight_copy(a, j).wait()
        if a == 0:
            return lax.dot_general(cot_all[...], wdown[j], contract_last, preferred_element_type=f32)
        w = wgate if a == 1 else wup
        return jnp.dot(tok_all[...], w[j], preferred_element_type=f32)

    for a in range(3):
        def step(j, carry, a=a):
            value = partial(a, j)
            own[a] = value

            @pl.when(j < C - 1)
            def _():
                if a == 0:
                    gh_out[j] = value.astype(bf16)
                else:
                    part32[a - 1, j] = value
                part_copy(a, j).start()
            return carry
        lax.fori_loop(0, C, step, 0)

    for k in range(1, C):
        m_copy(k).wait_recv()
    pick = one_hot(T, C * 16, lambda i, j: j == (i // tm) * 16 + i % tm)
    keep = jnp.dot(pick, mall[...].reshape(C * 16, S), preferred_element_type=f32) * keep_scale
    gh = own[0]
    for j in range(C - 1):
        part_copy(0, j).wait_recv()
    for k in range(1, C):
        gh = gh + gh_in[lax.rem(me_c + k, C)].astype(f32)
    gate = own[1]
    for j in range(C - 1):
        part_copy(1, j).wait_recv()
    for k in range(1, C):
        gate = gate + gu_in[0, lax.rem(me_c + k, C)]
    up = own[2]
    for j in range(C - 1):
        part_copy(2, j).wait_recv()
    for k in range(1, C):
        up = up + gu_in[1, lax.rem(me_c + k, C)]
    sig = 1.0 / (1.0 + jnp.exp(-gate))
    silu = gate * sig
    pre = gh * keep
    act[me_c, 0] = (silu * up * keep).astype(bf16)
    act[me_c, 1] = (pre * up * sig * (1.0 + gate * (1.0 - sig))).astype(bf16)
    act[me_c, 2] = (pre * silu).astype(bf16)

    def act_copy(k):
        return pltpu.make_async_remote_copy(
            src_ref=act.at[me_c], dst_ref=act.at[me_c], send_sem=a_send.at[k], recv_sem=a_recv.at[k],
            device_id={"col": lax.rem(me_c + k, C)}, device_id_type=MESH)

    for k in range(1, C):
        act_copy(k).start()

    spread = one_hot(R * 8, T, lambda i, j: (j == (i // 8) * t + i % 8) & (i % 8 < t))
    acc[...] = jnp.zeros_like(acc)

    def widen(value):
        return jnp.dot(spread, value, preferred_element_type=f32).astype(bf16)

    def back(k, carry):
        p = lax.rem(me_c + C - k, C)
        j = C - 1 - k

        @pl.when(k > 0)
        def _():
            act_copy(k).wait_recv()
        acc[0] += jnp.dot(widen(act[p, 0]), wdown[j], preferred_element_type=f32)
        acc[1] += lax.dot_general(
            widen(act[p, 1]), wgate[j], contract_last, preferred_element_type=f32
        ) + lax.dot_general(widen(act[p, 2]), wup[j], contract_last, preferred_element_type=f32)
        return carry
    lax.fori_loop(0, C, back, 0)

    def r_copy(k):
        p = lax.rem(me_r + k, R)
        return pltpu.make_async_remote_copy(
            src_ref=rs_out.at[k], dst_ref=rs_in.at[me_r], send_sem=r_send.at[k], recv_sem=r_recv.at[k],
            device_id={"row": p}, device_id_type=MESH)

    def rows(p):
        return pl.ds(pl.multiple_of(p * 8, 8), 8)

    for k in range(1, R):
        p = lax.rem(me_r + k, R)
        rs_out[k] = jnp.concatenate([acc[0, rows(p), :], acc[1, rows(p), :]], axis=0).astype(bf16)
        r_copy(k).start()
    total = jnp.concatenate([acc[0, rows(me_r), :], acc[1, rows(me_r), :]], axis=0)
    for k in range(1, R):
        r_copy(k).wait_recv()
    for k in range(1, R):
        total = total + rs_in[lax.rem(me_r + k, R)].astype(f32)
    mixed_ref[...] = total[0:t].astype(bf16)
    input_ref[...] = total[8:8 + t].astype(bf16)

    for k in range(1, R):
        x_copy(k).wait_send()
        r_copy(k).wait_send()
    for k in range(1, C):
        m_copy(k).wait_send()
        act_copy(k).wait_send()
    for a in range(3):
        for j in range(C - 1):
            part_copy(a, j).wait_send()


def outer_kernel(tok_ref, cot_ref, act_ref, gate_out, up_out, down_out):
    tok = tok_ref[...]
    gate_out[...] = lax.dot_general(
        tok, act_ref[0, 1], contract_first, preferred_element_type=f32).astype(bf16)
    up_out[...] = lax.dot_general(
        tok, act_ref[0, 2], contract_first, preferred_element_type=f32).astype(bf16)
    down_out[...] = lax.dot_general(
        act_ref[0, 0], cot_ref[...], contract_first, preferred_element_type=f32).astype(bf16)


def kernel_body(R, C, tokens, gate_weight, up_weight, down_weight, keep_mask, cotangent):
    t, D = tokens.shape
    F = gate_weight.shape[1]
    S = F // C
    T = R * t
    vm = pl.BlockSpec(memory_space=pltpu.VMEM)
    anyspec = pl.BlockSpec(memory_space=pl.ANY)
    dma = pltpu.SemaphoreType.DMA
    sds = jax.ShapeDtypeStruct
    V = pltpu.VMEM
    mixed, input_grad, tok_all, cot_all, act = pl.pallas_call(
        functools.partial(layer_kernel, R, C),
        name="layer",
        out_shape=(sds((t, D), bf16), sds((t, D), bf16), sds((T, D), bf16), sds((T, D), bf16),
                   sds((C, 3, T, S), bf16)),
        in_specs=[vm, vm, vm, anyspec, anyspec, anyspec],
        out_specs=(vm,) * 5,
        scratch_shapes=[
            V((C, D, S), bf16), V((C, D, S), bf16), V((C, S, D), bf16), dma((3, C)),
            V((16, D), f32), V((16, D), bf16), V((R, 16, D), bf16), dma((R,)), dma((R,)),
            V((16, F), f32), V((16, F), bf16), V((C, 16, S), bf16), dma((C,)), dma((C,)),
            V((2, C, T, S), f32), V((3, T, S), f32), V((C, T, S), bf16), V((C, T, S), bf16),
            V((2, C, T, S), f32), dma((3, C)), dma((3, C)),
            dma((C,)), dma((C,)), V((2, R * 8, D), f32), V((R, 16, D), bf16), V((R, 16, D), bf16),
            dma((R,)), dma((R,)),
        ],
        compiler_params=pltpu.CompilerParams(
            collective_id=0, has_side_effects=True, vmem_limit_bytes=60 * 1024 * 1024),
    )(tokens, cotangent, keep_mask, gate_weight, up_weight, down_weight)
    split = 2 if D % 256 == 0 else 1
    H = D // split
    gate_grad, up_grad, down_grad = pl.pallas_call(
        outer_kernel,
        name="outer",
        grid=(C, split),
        out_shape=(sds((D, F), bf16), sds((D, F), bf16), sds((F, D), bf16)),
        in_specs=[
            pl.BlockSpec((T, H), lambda p, h: (0, h)),
            pl.BlockSpec((T, H), lambda p, h: (0, h)),
            pl.BlockSpec((1, 3, T, S), lambda p, h: (p, 0, 0, 0)),
        ],
        out_specs=(
            pl.BlockSpec((H, S), lambda p, h: (h, p)),
            pl.BlockSpec((H, S), lambda p, h: (h, p)),
            pl.BlockSpec((S, H), lambda p, h: (p, h)),
        ),
        compiler_params=pltpu.CompilerParams(vmem_limit_bytes=40 * 1024 * 1024),
    )(tok_all, cot_all, act)
    return mixed, input_grad, gate_grad, up_grad, down_grad


def body(R, C, tokens, gate_weight, up_weight, down_weight, keep_mask, cotangent):
    t, D = tokens.shape
    F = gate_weight.shape[1]
    tm = keep_mask.shape[0]
    fits = t <= 8 and tm <= 16 and F % (C * 128) == 0 and D % 128 == 0
    if fits:
        return kernel_body(R, C, tokens, gate_weight, up_weight, down_weight, keep_mask, cotangent)
    return plain_body(tokens, gate_weight, up_weight, down_weight, keep_mask, cotangent)


def solution(mesh):
    placed = (
        P("row", "col"),
        P("col", "row"),
        P("col", "row"),
        P("row", "col"),
        P("col", "row"),
        P("row", "col"),
    )
    return jax.shard_map(
        functools.partial(body, mesh.shape["row"], mesh.shape["col"]),
        mesh=mesh,
        in_specs=placed,
        out_specs=(
            P("row", "col"),
            P("row", "col"),
            P("col", "row"),
            P("col", "row"),
            P("row", "col"),
        ),
        check_vma=False,
    )
```

time: 220 us -> 91.6 us (0.42)
  the two profiles are of different devices: /device:TPU:0 before, /device:TPU:29 now
where the time goes in v1:
time: 91.6 us; the launch traced here: 91.2 us
  Pallas kernels  84.8 us (93%)
  local copies, waits for them, and re-layouts  5.71 us (6%)
    pallas_call x1, Pallas kernels, kernel_body(): pl.pallas_call(functools.partial(layer_kernel, R, C), name='layer', out_s...  72.5 us
    pallas_call x1, Pallas kernels, kernel_body(): pl.pallas_call(outer_kernel, name='outer', grid=(C, split), out_shape=(sd...  12.3 us
    unnamed x8, local copies, waits for them, and re-layouts  5.71 us

profile of v1, /device:TPU:29, one launch (start us, length us, event | category | flops | bytes accessed | tf_op | source)
XLA Modules:
  0.0 91.2 jit_solution(13386582274599151598)
XLA Ops:
  0.6 72.5 %layer.1 = (bf16[6,2048]{1,0:T(8,128)(2,1)}, bf16[6,2048]{1,0:T(8,128)(2,1)}, bf16[48,2048]{1,0:T(8,128)(2,1)}, bf16[48,2048]{1,0:T(8,128)(2,1)}, bf16[4,3,48,640]{3,2,1,0:T(8,128)(2,1)}) custom-call(bf16[6,2048]{1,0:T(8,128)(2,1)} %tok_ref.1, bf16[6,2048]{1,0:T(8,128)(2,1)} %cot_ref.1, s32[12,2560]{1,0:T(8,128)} %mask_ref.1, bf16[2048,2560]{1,0:T(8,128)(2,1)} %gate_hbm.1, ...), custom_call_target="tpu_custom_call" | custom-call | tf_op jit(solution)/shard_map/layer/pallas_call | solution.py:278
  73.2 0.0 copy-start
  73.2 1.1 %copy-done = bf16[4,3,48,640]{3,2,1,0:T(8,128)(2,1)S(1)} copy-done((bf16[4,3,48,640]{3,2,1,0:T(8,128)(2,1)S(1)}, bf16[4,3,48,640]{3,2,1,0:T(8,128)(2,1)}, u32[]{:S(2)}) %copy-start) | copy-done | bytes 737304
  74.3 0.0 copy-start.1
  74.3 0.9 %copy-done.1 = bf16[48,2048]{1,0:T(8,128)(2,1)S(1)} copy-done((bf16[48,2048]{1,0:T(8,128)(2,1)S(1)}, bf16[48,2048]{1,0:T(8,128)(2,1)}, u32[]{:S(2)}) %copy-start.1) | copy-done | bytes 196632
  75.2 0.0 copy-start.2
  75.2 0.9 %copy-done.2 = bf16[48,2048]{1,0:T(8,128)(2,1)S(1)} copy-done((bf16[48,2048]{1,0:T(8,128)(2,1)S(1)}, bf16[48,2048]{1,0:T(8,128)(2,1)}, u32[]{:S(2)}) %copy-start.2) | copy-done | bytes 196632
  76.2 12.3 %outer.1 = (bf16[2048,2560]{1,0:T(8,128)(2,1)}, bf16[2048,2560]{1,0:T(8,128)(2,1)}, bf16[2560,2048]{1,0:T(8,128)(2,1)}) custom-call(bf16[48,2048]{1,0:T(8,128)(2,1)S(1)} %copy-done.1, bf16[48,2048]{1,0:T(8,128)(2,1)S(1)} %copy-done.2, bf16[4,3,48,640]{3,2,1,0:T(8,128)(2,1)S(1)} %copy-done), custom_call_target="tpu_custom_call" | custom-call | tf_op jit(solution)/shard_map/outer/pallas_call | solution.py:299
  88.4 1.4 %copy.13 = bf16[6,2048]{1,0:T(8,128)(2,1)} copy(bf16[6,2048]{1,0:T(8,128)(2,1)} %get-tuple-element.26) | data formatting | bytes 49152
  89.8 1.4 %copy.14 = bf16[6,2048]{1,0:T(8,128)(2,1)} copy(bf16[6,2048]{1,0:T(8,128)(2,1)} %get-tuple-element.27) | data formatting | bytes 49152
Async XLA Ops:
  73.2 1.1 %copy-start = (bf16[4,3,48,640]{3,2,1,0:T(8,128)(2,1)S(1)}, bf16[4,3,48,640]{3,2,1,0:T(8,128)(2,1)}, u32[]{:S(2)}) copy-start(bf16[4,3,48,640]{3,2,1,0:T(8,128)(2,1)} %get-tuple-element.17.act_ref) | copy-start | bytes 2211844
  74.3 0.9 %copy-start.1 = (bf16[48,2048]{1,0:T(8,128)(2,1)S(1)}, bf16[48,2048]{1,0:T(8,128)(2,1)}, u32[]{:S(2)}) copy-start(bf16[48,2048]{1,0:T(8,128)(2,1)} %get-tuple-element.15.tok_ref) | copy-start | bytes 589828
  75.2 0.9 %copy-start.2 = (bf16[48,2048]{1,0:T(8,128)(2,1)S(1)}, bf16[48,2048]{1,0:T(8,128)(2,1)}, u32[]{:S(2)}) copy-start(bf16[48,2048]{1,0:T(8,128)(2,1)} %get-tuple-element.16.cot_ref) | copy-start | bytes 589828

commit v2 on v1

--- a/solution.py
+++ b/solution.py
@@ -71,7 +71,7 @@
                  mixed_ref, input_ref, tok_all, cot_all, act,
                  wgate, wup, wdown, wsem, pack, packed, gathered, x_send, x_recv,
                  mpad, mpacked, mall, m_send, m_recv,
-                 part32, own, gh_out, gh_in, gu_in, p_send, p_recv,
+                 part32, own, part16, pair_in, gate_in, p_send, p_recv,
                  a_send, a_recv, acc, rs_out, rs_in, r_send, r_recv):
     me_r = lax.axis_index("row")
     me_c = lax.axis_index("col")
@@ -89,8 +89,8 @@
 
     def weight_copy(a, j):
         p = peer_c(j)
-        src, dst = ((down_hbm.at[cols(p), :], wdown), (gate_hbm.at[:, cols(p)], wgate),
-                    (up_hbm.at[:, cols(p)], wup))[a]
+        src, dst = ((gate_hbm.at[:, cols(p)], wgate), (up_hbm.at[:, cols(p)], wup),
+                    (down_hbm.at[cols(p), :], wdown))[a]
         return pltpu.make_async_copy(src, dst.at[j], wsem.at[a, j])
 
     for a in range(3):
@@ -141,17 +141,19 @@
     cot_all[...] = jnp.dot(pick, flat, preferred_element_type=f32).astype(bf16)
 
     def part_copy(a, j):
-        src, dst = ((gh_out.at[j], gh_in.at[me_c]), (part32.at[0, j], gu_in.at[0, me_c]),
-                    (part32.at[1, j], gu_in.at[1, me_c]))[a]
+        if a == 0:
+            src, dst = part32.at[j], gate_in.at[me_c]
+        else:
+            src, dst = part16.at[a - 1, j], pair_in.at[a - 1, me_c]
         return pltpu.make_async_remote_copy(
             src_ref=src, dst_ref=dst, send_sem=p_send.at[a, j], recv_sem=p_recv.at[a, j],
             device_id={"col": peer_c(j)}, device_id_type=MESH)
 
     def partial(a, j):
         weight_copy(a, j).wait()
-        if a == 0:
+        if a == 2:
             return lax.dot_general(cot_all[...], wdown[j], contract_last, preferred_element_type=f32)
-        w = wgate if a == 1 else wup
+        w = wgate if a == 0 else wup
         return jnp.dot(tok_all[...], w[j], preferred_element_type=f32)
 
     for a in range(3):
@@ -162,9 +164,9 @@
             @pl.when(j < C - 1)
             def _():
                 if a == 0:
-                    gh_out[j] = value.astype(bf16)
+                    part32[j] = value
                 else:
-                    part32[a - 1, j] = value
+                    part16[a - 1, j] = value.astype(bf16)
                 part_copy(a, j).start()
             return carry
         lax.fori_loop(0, C, step, 0)
@@ -173,35 +175,33 @@
         m_copy(k).wait_recv()
     pick = one_hot(T, C * 16, lambda i, j: j == (i // tm) * 16 + i % tm)
     keep = jnp.dot(pick, mall[...].reshape(C * 16, S), preferred_element_type=f32) * keep_scale
-    gh = own[0]
-    for j in range(C - 1):
-        part_copy(0, j).wait_recv()
-    for k in range(1, C):
-        gh = gh + gh_in[lax.rem(me_c + k, C)].astype(f32)
-    gate = own[1]
-    for j in range(C - 1):
-        part_copy(1, j).wait_recv()
-    for k in range(1, C):
-        gate = gate + gu_in[0, lax.rem(me_c + k, C)]
-    up = own[2]
-    for j in range(C - 1):
-        part_copy(2, j).wait_recv()
-    for k in range(1, C):
-        up = up + gu_in[1, lax.rem(me_c + k, C)]
+    def act_copy(n, k):
+        return pltpu.make_async_remote_copy(
+            src_ref=act.at[me_c, n], dst_ref=act.at[me_c, n], send_sem=a_send.at[n, k],
+            recv_sem=a_recv.at[n, k], device_id={"col": lax.rem(me_c + k, C)}, device_id_type=MESH)
+
+    def summed(a):
+        value = own[a]
+        for j in range(C - 1):
+            part_copy(a, j).wait_recv()
+        for k in range(1, C):
+            p = lax.rem(me_c + k, C)
+            value = value + (gate_in[p] if a == 0 else pair_in[a - 1, p].astype(f32))
+        return value
+
+    gate = summed(0)
+    up = summed(1)
     sig = 1.0 / (1.0 + jnp.exp(-gate))
     silu = gate * sig
-    pre = gh * keep
     act[me_c, 0] = (silu * up * keep).astype(bf16)
+    for k in range(1, C):
+        act_copy(0, k).start()
+    pre = summed(2) * keep
     act[me_c, 1] = (pre * up * sig * (1.0 + gate * (1.0 - sig))).astype(bf16)
     act[me_c, 2] = (pre * silu).astype(bf16)
-
-    def act_copy(k):
-        return pltpu.make_async_remote_copy(
-            src_ref=act.at[me_c], dst_ref=act.at[me_c], send_sem=a_send.at[k], recv_sem=a_recv.at[k],
-            device_id={"col": lax.rem(me_c + k, C)}, device_id_type=MESH)
-
-    for k in range(1, C):
-        act_copy(k).start()
+    for n in (1, 2):
+        for k in range(1, C):
+            act_copy(n, k).start()
 
     spread = one_hot(R * 8, T, lambda i, j: (j == (i // 8) * t + i % 8) & (i % 8 < t))
     acc[...] = jnp.zeros_like(acc)
@@ -209,53 +209,77 @@
     def widen(value):
         return jnp.dot(spread, value, preferred_element_type=f32).astype(bf16)
 
-    def back(k, carry):
+    def back_mixed(k, carry):
+        p = lax.rem(me_c + C - k, C)
+
+        @pl.when(k > 0)
+        def _():
+            act_copy(0, k).wait_recv()
+        acc[0] += jnp.dot(widen(act[p, 0]), wdown[C - 1 - k], preferred_element_type=f32)
+        return carry
+
+    def back_input(k, carry):
         p = lax.rem(me_c + C - k, C)
         j = C - 1 - k
 
         @pl.when(k > 0)
         def _():
-            act_copy(k).wait_recv()
-        acc[0] += jnp.dot(widen(act[p, 0]), wdown[j], preferred_element_type=f32)
+            act_copy(1, k).wait_recv()
         acc[1] += lax.dot_general(
-            widen(act[p, 1]), wgate[j], contract_last, preferred_element_type=f32
-        ) + lax.dot_general(widen(act[p, 2]), wup[j], contract_last, preferred_element_type=f32)
+            widen(act[p, 1]), wgate[j], contract_last, preferred_element_type=f32)
+
+        @pl.when(k > 0)
+        def _():
+            act_copy(2, k).wait_recv()
+        acc[1] += lax.dot_general(
+            widen(act[p, 2]), wup[j], contract_last, preferred_element_type=f32)
         return carry
-    lax.fori_loop(0, C, back, 0)
-
-    def r_copy(k):
-        p = lax.rem(me_r + k, R)
-        return pltpu.make_async_remote_copy(
-            src_ref=rs_out.at[k], dst_ref=rs_in.at[me_r], send_sem=r_send.at[k], recv_sem=r_recv.at[k],
-            device_id={"row": p}, device_id_type=MESH)
+
+    def r_copy(n, k):
+        return pltpu.make_async_remote_copy(
+            src_ref=rs_out.at[n, k], dst_ref=rs_in.at[n, me_r], send_sem=r_send.at[n, k],
+            recv_sem=r_recv.at[n, k], device_id={"row": lax.rem(me_r + k, R)}, device_id_type=MESH)
 
     def rows(p):
         return pl.ds(pl.multiple_of(p * 8, 8), 8)
 
-    for k in range(1, R):
-        p = lax.rem(me_r + k, R)
-        rs_out[k] = jnp.concatenate([acc[0, rows(p), :], acc[1, rows(p), :]], axis=0).astype(bf16)
-        r_copy(k).start()
-    total = jnp.concatenate([acc[0, rows(me_r), :], acc[1, rows(me_r), :]], axis=0)
-    for k in range(1, R):
-        r_copy(k).wait_recv()
-    for k in range(1, R):
-        total = total + rs_in[lax.rem(me_r + k, R)].astype(f32)
-    mixed_ref[...] = total[0:t].astype(bf16)
-    input_ref[...] = total[8:8 + t].astype(bf16)
+    def send_rows(n):
+        for k in range(1, R):
+            rs_out[n, k] = acc[n, rows(lax.rem(me_r + k, R)), :].astype(bf16)
+            r_copy(n, k).start()
+
+    def sum_rows(n):
+        total = acc[n, rows(me_r), :]
+        for k in range(1, R):
+            r_copy(n, k).wait_recv()
+        for k in range(1, R):
+            total = total + rs_in[n, lax.rem(me_r + k, R)].astype(f32)
+        return total[0:t].astype(bf16)
+
+    lax.fori_loop(0, C, back_mixed, 0)
+    send_rows(0)
+    lax.fori_loop(0, C, back_input, 0)
+    send_rows(1)
+    mixed_ref[...] = sum_rows(0)
+    input_ref[...] = sum_rows(1)
 
     for k in range(1, R):
         x_copy(k).wait_send()
-        r_copy(k).wait_send()
+        r_copy(0, k).wait_send()
+        r_copy(1, k).wait_send()
     for k in range(1, C):
         m_copy(k).wait_send()
-        act_copy(k).wait_send()
+        for n in range(3):
+            act_copy(n, k).wait_send()
     for a in range(3):
         for j in range(C - 1):
             part_copy(a, j).wait_send()
 
 
-def outer_kernel(tok_ref, cot_ref, act_ref, gate_out, up_out, down_out):
+def outer_kernel(tok_ref, cot_ref, act_ref, mixed_ref, input_ref,
+                 gate_out, up_out, down_out, mixed_out, input_out):
+    mixed_out[...] = mixed_ref[...]
+    input_out[...] = input_ref[...]
     tok = tok_ref[...]
     gate_out[...] = lax.dot_general(
         tok, act_ref[0, 1], contract_first, preferred_element_type=f32).astype(bf16)
@@ -286,33 +310,37 @@
             V((C, D, S), bf16), V((C, D, S), bf16), V((C, S, D), bf16), dma((3, C)),
             V((16, D), f32), V((16, D), bf16), V((R, 16, D), bf16), dma((R,)), dma((R,)),
             V((16, F), f32), V((16, F), bf16), V((C, 16, S), bf16), dma((C,)), dma((C,)),
-            V((2, C, T, S), f32), V((3, T, S), f32), V((C, T, S), bf16), V((C, T, S), bf16),
-            V((2, C, T, S), f32), dma((3, C)), dma((3, C)),
-            dma((C,)), dma((C,)), V((2, R * 8, D), f32), V((R, 16, D), bf16), V((R, 16, D), bf16),
-            dma((R,)), dma((R,)),
+            V((C, T, S), f32), V((3, T, S), f32), V((2, C, T, S), bf16), V((2, C, T, S), bf16),
+            V((C, T, S), f32), dma((3, C)), dma((3, C)),
+            dma((3, C)), dma((3, C)), V((2, R * 8, D), f32), V((2, R, 8, D), bf16),
+            V((2, R, 8, D), bf16), dma((2, R)), dma((2, R)),
         ],
         compiler_params=pltpu.CompilerParams(
             collective_id=0, has_side_effects=True, vmem_limit_bytes=60 * 1024 * 1024),
     )(tokens, cotangent, keep_mask, gate_weight, up_weight, down_weight)
     split = 2 if D % 256 == 0 else 1
     H = D // split
-    gate_grad, up_grad, down_grad = pl.pallas_call(
+    whole = pl.BlockSpec((t, D), lambda p, h: (0, 0))
+    gate_grad, up_grad, down_grad, mixed, input_grad = pl.pallas_call(
         outer_kernel,
         name="outer",
         grid=(C, split),
-        out_shape=(sds((D, F), bf16), sds((D, F), bf16), sds((F, D), bf16)),
+        out_shape=(sds((D, F), bf16), sds((D, F), bf16), sds((F, D), bf16),
+                   sds((t, D), bf16), sds((t, D), bf16)),
         in_specs=[
             pl.BlockSpec((T, H), lambda p, h: (0, h)),
             pl.BlockSpec((T, H), lambda p, h: (0, h)),
             pl.BlockSpec((1, 3, T, S), lambda p, h: (p, 0, 0, 0)),
+            whole, whole,
         ],
         out_specs=(
             pl.BlockSpec((H, S), lambda p, h: (h, p)),
             pl.BlockSpec((H, S), lambda p, h: (h, p)),
             pl.BlockSpec((S, H), lambda p, h: (p, h)),
+            whole, whole,
         ),
-        compiler_params=pltpu.CompilerParams(vmem_limit_bytes=40 * 1024 * 1024),
-    )(tok_all, cot_all, act)
+        compiler_params=pltpu.CompilerParams(vmem_limit_bytes=63 * 1024 * 1024),
+    )(tok_all, cot_all, act, mixed, input_grad)
     return mixed, input_grad, gate_grad, up_grad, down_grad
 
 

time: 91.6 us -> 76.3 us (0.83)
  the two profiles are of different devices: /device:TPU:29 before, /device:TPU:0 now
where the time goes in v2:
time: 76.3 us; the launch traced here: 76.1 us
  Pallas kernels  75.4 us (99%)
    pallas_call x1, Pallas kernels, kernel_body(): pl.pallas_call(functools.partial(layer_kernel, R, C), name='layer', out_s...  62.1 us
    pallas_call x1, Pallas kernels, kernel_body(): pl.pallas_call(outer_kernel, name='outer', grid=(C, split), out_shape=(sd...  13.3 us

profile of v2, /device:TPU:0, one launch (start us, length us, event | category | flops | bytes accessed | tf_op | source)
XLA Modules:
  0.0 76.1 jit_solution(5212494858025085630)
XLA Ops:
  0.6 62.1 %layer.1 = (bf16[6,2048]{1,0:T(8,128)(2,1)}, bf16[6,2048]{1,0:T(8,128)(2,1)}, bf16[48,2048]{1,0:T(8,128)(2,1)}, bf16[48,2048]{1,0:T(8,128)(2,1)}, bf16[4,3,48,640]{3,2,1,0:T(8,128)(2,1)}) custom-call(bf16[6,2048]{1,0:T(8,128)(2,1)} %tok_ref.1, bf16[6,2048]{1,0:T(8,128)(2,1)} %cot_ref.1, s32[12,2560]{1,0:T(8,128)} %mask_ref.1, bf16[2048,2560]{1,0:T(8,128)(2,1)} %gate_hbm.1, ...), custom_call_target="tpu_custom_call" | custom-call | tf_op jit(solution)/shard_map/layer/pallas_call | solution.py:302
  62.8 13.3 %outer.1 = (bf16[2048,2560]{1,0:T(8,128)(2,1)}, bf16[2048,2560]{1,0:T(8,128)(2,1)}, bf16[2560,2048]{1,0:T(8,128)(2,1)}, bf16[6,2048]{1,0:T(8,128)(2,1)}, bf16[6,2048]{1,0:T(8,128)(2,1)}) custom-call(bf16[48,2048]{1,0:T(8,128)(2,1)} %get-tuple-element.15.tok_ref, bf16[48,2048]{1,0:T(8,128)(2,1)} %get-tuple-element.16.cot_ref, ...), custom_call_target="tpu_custom_call" | custom-call | tf_op jit(solution)/shard_map/outer/pallas_call | solution.py:324
